TPU v7x, 512 devices: a whole 4x8x8 slice. The times are simulated.
512 devices in a mesh: dp: 16 (over y_lo, x), space: 32 (over z, y_hi, core).
Axes of the slice: x: 4, y: 8 (y_hi: 2, y_lo: 4; y = y_hi * 4 + y_lo), z: 8, core: 2. Of those that a mesh axis runs over, the one named last changes fastest.
Arguments:
- fields: bfloat16 [16, 100, 131072], P('dp', None, 'space'), may hold values from -6 to 6
- cell_index: int32 [1024, 128], P('space'), may hold values from 0 to 6143
- interp_weight: bfloat16 [1024, 16, 128], P('space'), may hold values from 0 to 2, as said below
- w_in: bfloat16 [100, 1024], replicated, may hold values from -0.625 to 0.625
- ln_gain: float32 [1024], replicated, may hold values from 0.5 to 1.5
- w_qkv: bfloat16 [1024, 3072], P('dp'), may hold values from -0.1875 to 0.1875
- w_out: bfloat16 [1024, 1024], P('dp'), may hold values from -3 to 3
Outputs:
- latent: bfloat16 [16, 16384, 1024], P('dp', 'space')
- update: bfloat16 [16, 16384, 1024], P('dp', 'space')
Inputs may be any that keep to these rules, and one draw needn't show every extreme that they name: `interp_weight`: in each block the slots from some count on carry zero weight for all its 16 nodes; that count lies between 48 and 128. `cell_index`: indexes a shard's 4096 cells extended by 1024 cells of each neighbouring shard, lower neighbour first.
All inputs are finite; a program needn't handle non-finite values.
Results may differ from a plain program's by a relative error of at most 0.0068.
Values may be sent and summed in bfloat16 or wider, within the bound.
A program may use at most 128 MiB of HBM per device.

v0:
```python
import math
import jax
import jax.numpy as jnp
from jax import lax
from jax.sharding import PartitionSpec as P

HEADS = 16


def padded(array, sides, width):
    for axis, dim in sides:
        size, length = (lax.axis_size(axis), array.shape[dim])
        up = [(i, (i + 1) % size) for i in range(size)]
        down = [(j, i) for i, j in up]
        last = lax.slice_in_dim(array, length - width, length, axis=dim)
        first = lax.slice_in_dim(array, 0, width, axis=dim)
        before = lax.ppermute(last, axis, up)
        after = lax.ppermute(first, axis, down)
        array = jnp.concatenate([before, array, after], axis=dim)
    return array


def unit_heads(projected):
    head_size = projected.shape[1] // HEADS
    head_rows = projected.reshape(projected.shape[0], HEADS, head_size)
    scale_rows = jnp.sqrt(jnp.mean(head_rows * head_rows, axis=-1, keepdims=True) + 1e-06)
    return (head_rows / scale_rows).astype(jnp.bfloat16).reshape(projected.shape)


def shards(fields, cell_index, interp_weight, w_in, ln_gain, w_qkv, w_out):
    width = w_qkv.shape[1] // 3
    full_qkv, full_out = (
        lax.all_gather(w_qkv, "dp", axis=0, tiled=True),
        lax.all_gather(w_out, "dp", axis=0, tiled=True),
    )
    grid_field = fields[0]
    cell_count = grid_field.shape[1]
    cell_reach = cell_count // 4
    extended = padded(grid_field, (("space", 1),), cell_reach)
    picked = jnp.take(extended, cell_index, axis=1)
    encoded = jnp.einsum("cbs,bns->bnc", picked, interp_weight, preferred_element_type=jnp.float32)
    node_count = encoded.shape[0] * encoded.shape[1]
    encoded = encoded.reshape(node_count, encoded.shape[2]).astype(jnp.bfloat16)
    embedded = jnp.dot(encoded, w_in, preferred_element_type=jnp.float32)
    average = jnp.mean(embedded, axis=1, keepdims=True)
    centered = embedded - average
    spread = jnp.mean(centered * centered, axis=1, keepdims=True)
    normed = (centered / jnp.sqrt(spread + 1e-05) * ln_gain).astype(jnp.bfloat16)
    margin = node_count // 2
    bordered = padded(normed, (("space", 0),), margin)
    side_normed = jnp.concatenate([bordered[:margin], bordered[margin + node_count :]], axis=0)
    projected = jnp.dot(normed, full_qkv, preferred_element_type=jnp.float32)
    side_projected = jnp.dot(side_normed, full_qkv[:, width:], preferred_element_type=jnp.float32)
    queries = unit_heads(projected[:, :width])
    own_pairs = jnp.concatenate(
        [
            unit_heads(projected[:, width : 2 * width]),
            projected[:, 2 * width :].astype(jnp.bfloat16),
        ],
        axis=1,
    )
    side_pairs = jnp.concatenate(
        [unit_heads(side_projected[:, :width]), side_projected[:, width:].astype(jnp.bfloat16)],
        axis=1,
    )
    window = jnp.concatenate([side_pairs[:margin], own_pairs, side_pairs[margin:]], axis=0)
    head_size = width // HEADS
    group_width = 2 * head_size

    def attend(group_index):
        offset = group_index * group_width
        query_group = lax.dynamic_slice_in_dim(queries, offset, group_width, 1).reshape(
            node_count, 2, head_size
        )
        key_group = lax.dynamic_slice_in_dim(window, offset, group_width, 1).reshape(
            window.shape[0], 2, head_size
        )
        value_group = lax.dynamic_slice_in_dim(window, width + offset, group_width, 1).reshape(
            window.shape[0], 2, head_size
        )
        scores = jnp.einsum(
            "qhd,khd->hqk", query_group, key_group, preferred_element_type=jnp.float32
        ) / math.sqrt(head_size)
        weights = jnp.exp(scores)
        probs = (weights / jnp.sum(weights, axis=2, keepdims=True)).astype(jnp.bfloat16)
        mixed_rows = jnp.einsum(
            "hqk,khd->qhd", probs, value_group, preferred_element_type=jnp.float32
        )
        return mixed_rows.astype(jnp.bfloat16).reshape(node_count, group_width)

    grouped = lax.map(attend, jnp.arange(HEADS // 2, dtype=jnp.int32))
    attended = grouped.transpose(1, 0, 2).reshape(node_count, width)
    update = jnp.dot(attended, full_out, preferred_element_type=jnp.float32)
    return (embedded.astype(jnp.bfloat16)[None], update.astype(jnp.bfloat16)[None])


def solution(mesh):
    placed = (
        P("dp", None, "space"),
        P("space", None),
        P("space", None, None),
        P(),
        P(),
        P("dp", None),
        P("dp", None),
    )
    return jax.shard_map(
        shards,
        mesh=mesh,
        in_specs=placed,
        out_specs=(P("dp", "space", None), P("dp", "space", None)),
        check_vma=False,
    )
```

profile of v0, /device:TPU:256, one launch (start us, length us, event | category | flops | bytes accessed | tf_op | source)
XLA Modules:
  0.0 250.1 jit_solution(16279916706704496909)
XLA Ops:
  8.0 1.6 copy.13
  9.6 6.3 %collective-permute-start.1 = (bf16[100,1024]{0,1:T(8,128)(2,1)S(1)}, bf16[100,1024]{0,1:T(8,128)(2,1)S(1)}, u32[]{:S(2)}, u32[]{:S(2)}) collective-permute-start(bf16[100,1024]{0,1:T(8,128)(2,1)S(1)} %get-tuple-element.101), channel_id=1, source_target_pairs={{1,0},{2,1},{3,2},{4,3},{5,4},{6,5},{7,6},{8,7},{9,8},{10,9},{11,1... | collective-permute-start | bytes 614408 | tf_op jit(solution)/shard_map/ppermute | solution.py:18
  15.9 1.9 collective-permute-start
  17.9 2.6 %collective-permute-done.1 = bf16[100,1024]{0,1:T(8,128)(2,1)S(1)} collective-permute-done((bf16[100,1024]{0,1:T(8,128)(2,1)S(1)}, bf16[100,1024]{0,1:T(8,128)(2,1)S(1)}, u32[]{:S(2)}, u32[]{:S(2)}) %collective-permute-start.1) | collective-permute-done | bytes 204832 | tf_op jit(solution)/shard_map/ppermute | solution.py:18
  20.4 12.3 %collective-permute-done = bf16[100,1024]{0,1:T(8,128)(2,1)S(1)} collective-permute-done((bf16[100,1024]{0,1:T(8,128)(2,1)S(1)}, bf16[100,1024]{0,1:T(8,128)(2,1)S(1)}, u32[]{:S(2)}, u32[]{:S(2)}) %collective-permute-start) | collective-permute-done | bytes 204832 | tf_op jit(solution)/shard_map/ppermute | solution.py:17
  33.1 12.1 %gather_fusion = bf16[4096,100]{1,0:T(8,128)(2,1)S(1)} fusion(bf16[100,6144]{0,1:T(8,128)(2,1)S(1)} %pad_maximum_fusion, s32[4096]{0:T(1024)S(1)} %bitcast_clamp_fusion), kind=kCustom, calls=%fused_computation | custom fusion | bytes 1654784 | tf_op jit(solution)/shard_map/jit(_take)/gather | solution.py:40
  49.9 1.9 collective-permute-start.3
  51.8 2.6 %collective-permute-start.2 = (bf16[256,1024]{1,0:T(8,128)(2,1)S(1)}, bf16[256,1024]{1,0:T(8,128)(2,1)S(1)}, u32[]{:S(2)}, u32[]{:S(2)}) collective-permute-start(bf16[256,1024]{1,0:T(8,128)(2,1)S(1)} %get-tuple-element.98), channel_id=1, source_target_pairs={{0,1},{1,2},{2,3},{3,4},{4,5},{5,6},{6,7},{7,8},{8,9},{9,10},{10,1... | collective-permute-start | bytes 1572872 | tf_op jit(solution)/shard_map/ppermute | solution.py:17
  54.5 19.2 %collective-permute-done.3 = bf16[256,1024]{1,0:T(8,128)(2,1)S(1)} collective-permute-done((bf16[256,1024]{1,0:T(8,128)(2,1)S(1)}, bf16[256,1024]{1,0:T(8,128)(2,1)S(1)}, u32[]{:S(2)}, u32[]{:S(2)}) %collective-permute-start.3) | collective-permute-done | bytes 524320 | tf_op jit(solution)/shard_map/ppermute | solution.py:18
  73.7 8.8 %collective-permute-done.2 = bf16[256,1024]{1,0:T(8,128)(2,1)S(1)} collective-permute-done((bf16[256,1024]{1,0:T(8,128)(2,1)S(1)}, bf16[256,1024]{1,0:T(8,128)(2,1)S(1)}, u32[]{:S(2)}, u32[]{:S(2)}) %collective-permute-start.2) | collective-permute-done | bytes 524320 | tf_op jit(solution)/shard_map/ppermute | solution.py:17
  82.5 45.7 %all-gather.3.cloned.1.call-done = bf16[1024,3072]{1,0:T(8,128)(2,1)} async-done(((bf16[64,3072]{1,0:T(8,128)(2,1)}), bf16[1024,3072]{1,0:T(8,128)(2,1)}) %all-gather.3.cloned.1.call-update) | async-done | bytes 6291472 | tf_op jit(solution)/shard_map/all_gather | solution.py:33
  128.2 4.7 %fusion.8 = f32[512,2048]{1,0:T(8,128)S(1)} fusion(bf16[1024,3072]{1,0:T(8,128)(2,1)} %all-gather.3.cloned.1.call-done, bf16[256,1024]{1,0:T(8,128)(2,1)S(1)} %collective-permute-done.3, bf16[256,1024]{1,0:T(8,128)(2,1)S(1)} %collective-permute-done.2), kind=kOutput, calls=%fused_computation.16 | convolution fusion | flops 2149580800 | bytes 9437184 | tf_op jit(solution)/shard_map/dot_general | solution.py:53
  133.0 1.9 copy-done.3
  136.1 3.4 %fusion.24 = f32[512,3072]{1,0:T(8,128)S(1)} fusion(bf16[512,1024]{1,0:T(8,128)(2,1)S(1)} %copy-done.6, bf16[1024,3072]{1,0:T(8,128)(2,1)S(1)} %copy-done.10), kind=kOutput, calls=%fused_computation.59 | convolution fusion | flops 3221225472 | bytes 13631488 | tf_op jit(solution)/shard_map/dot_general | solution.py:52
  140.8 1.7 copy-done.2
  142.5 2.4 slice_multiply_fusion
  144.9 1.8 copy.15
  146.8 1.9 bitcast_reduce_fusion.2
  148.9 1.8 copy.16
  150.8 2.6 %divide_convert_fusion.6 = bf16[512,1024]{1,0:T(8,128)(2,1)S(1)} fusion(f32[512,1024]{1,0:T(8,128)} %copy.16, f32[512,2048]{1,0:T(8,128)} %copy-done.3), kind=kLoop, calls=%fused_computation.27 | loop fusion | flops 1048576 | bytes 5242880 | tf_op jit(solution)/shard_map/convert_element_type | solution.py:27
  153.4 2.9 %copy.19 = f32[512,1024]{0,1:T(8,128)} copy(f32[512,1024]{1,0:T(8,128)} %get-tuple-element.94) | data formatting | bytes 4194304 | tf_op jit(solution)/shard_map/mul | solution.py:26
  156.3 1.9 bitcast_reduce_fusion
  158.2 1.6 div.86
  159.9 2.9 %copy.20 = f32[512,1024]{1,0:T(8,128)} copy(f32[512,1024]{0,1:T(8,128)} %bitcast.62) | data formatting | bytes 4194304 | tf_op jit(solution)/shard_map/div | solution.py:27
  162.8 2.9 %copy.17 = f32[512,1024]{0,1:T(8,128)} copy(f32[512,1024]{1,0:T(8,128)} %get-tuple-element.95) | data formatting | bytes 4194304 | tf_op jit(solution)/shard_map/mul | solution.py:26
  165.7 1.9 bitcast_reduce_fusion.1
  169.2 2.9 %copy.18 = f32[512,1024]{1,0:T(8,128)} copy(f32[512,1024]{0,1:T(8,128)} %bitcast.63) | data formatting | bytes 4194304 | tf_op jit(solution)/shard_map/div | solution.py:27
  172.1 4.3 %divide_convert_fusion.4 = (bf16[512,1024]{1,0:T(8,128)(2,1)S(1)}, bf16[512,1024]{1,0:T(8,128)(2,1)S(1)}) fusion(f32[512,1024]{1,0:T(8,128)} %copy.20, f32[512,3072]{1,0:T(8,128)} %copy-done.2, f32[512,1024]{1,0:T(8,128)} %copy.18), kind=kLoop, calls=%fused_computation.25 | loop fusion | flops 2097152 | bytes 10485760 | tf_op jit(solution)/shard_map/convert_element_type | solution.py:27
  177.7 20.1 %fusion.7 = bf16[1024,2048]{1,0:T(8,128)(2,1)} fusion(bf16[512,1024]{1,0:T(8,128)(2,1)S(1)} %slice.81, bf16[512,1024]{1,0:T(8,128)(2,1)S(1)} %divide_convert_fusion.6, bf16[512,1024]{1,0:T(8,128)(2,1)S(1)} %copy-done.4, bf16[512,1024]{1,0:T(8,128)(2,1)S(1)} %get-tuple-element.93, bf16[256,2048]{1,0:T(8,128)(2,1)S(1)} %fusion.11), kind=kLoop, calls=%fused_computation.15 | loop fusion | flops 27262976 | bytes 9437184 | tf_op jit(solution)/shard_map/concatenate | solution.py:66
  197.8 6.5 %copy.21 = bf16[1024,2048]{0,1:T(8,128)(2,1)} copy(bf16[1024,2048]{1,0:T(8,128)(2,1)} %fusion.7) | data formatting | bytes 8388608 | tf_op jit(solution)/shard_map/while | solution.py:91
  204.3 34.9 %while.12 = (s32[]{:T(128)}, bf16[8,512,128]{1,2,0:T(8,128)(2,1)S(1)}, s32[8]{0:T(128)S(1)}, bf16[1024,2048]{0,1:T(8,128)(2,1)}, bf16[512,1024]{1,0:T(8,128)(2,1...) while((s32[]{:T(128)}, ...), condition=%wide.region_7.8_spmd, body=%wide.region_5.7_spmd.sunk | while | flops 273742848 | bytes 11018490 | solution.py:91
  239.3 3.9 %fusion.10 = bf16[1,512,1024]{2,1,0:T(8,128)(2,1)} fusion(bf16[512,1024]{0,1:T(8,128)(2,1)S(1)} %bitcast.69, bf16[1024,1024]{1,0:T(8,128)(2,1)} %all-gather.5.cloned.1.call-done), kind=kOutput, calls=%fused_computation.35 | convolution fusion | flops 1074266112 | bytes 4194304 | tf_op jit(solution)/shard_map/dot_general | solution.py:93
  (106 shorter events, 40.8 us)
Async XLA Ops:
  7.2 39.3 %copy-start = (bf16[100,1024]{1,0:T(8,128)(2,1)S(1)}, bf16[100,1024]{1,0:T(8,128)(2,1)}, u32[]{:S(2)}) copy-start(bf16[100,1024]{1,0:T(8,128)(2,1)} %param.12) | copy-start | bytes 614404
  7.2 10.7 %copy-start.8 = (s32[32,128]{1,0:T(8,128)S(1)}, s32[32,128]{1,0:T(8,128)}, u32[]{:S(2)}) copy-start(s32[32,128]{1,0:T(8,128)} %param.10) | copy-start | bytes 49156
  7.2 121.0 %all-gather.3.cloned.1.call-start = ((), (), s32[]{:S(2)}) async-start(), calls=%async_computation | async-start | bytes 6684672 | tf_op jit(solution)/shard_map/all_gather | solution.py:33
  7.9 231.4 %all-gather.5.cloned.1.call-start = ((), (), s32[]{:S(2)}) async-start(), calls=%async_computation.1 | async-start | bytes 2228224 | tf_op jit(solution)/shard_map/all_gather | solution.py:34
  9.6 10.8 %collective-permute-start.1 = (bf16[100,1024]{0,1:T(8,128)(2,1)S(1)}, bf16[100,1024]{0,1:T(8,128)(2,1)S(1)}, u32[]{:S(2)}, u32[]{:S(2)}) collective-permute-start(bf16[100,1024]{0,1:T(8,128)(2,1)S(1)} %get-tuple-element.101), channel_id=1, source_target_pairs={{1,0},{2,1},{3,2},{4,3},{5,4},{6,5},{7,6},{8,7},{9,8},{10,9},{11,1... | collective-permute-start | bytes 614408 | tf_op jit(solution)/shard_map/ppermute | solution.py:18
  15.9 16.8 %collective-permute-start = (bf16[100,1024]{0,1:T(8,128)(2,1)S(1)}, bf16[100,1024]{0,1:T(8,128)(2,1)S(1)}, u32[]{:S(2)}, u32[]{:S(2)}) collective-permute-start(bf16[100,1024]{0,1:T(8,128)(2,1)S(1)} %get-tuple-element.100), channel_id=1, source_target_pairs={{0,1},{1,2},{2,3},{3,4},{4,5},{5,6},{6,7},{7,8},{8,9},{9,10},{10,1... | collective-permute-start | bytes 614408 | tf_op jit(solution)/shard_map/ppermute | solution.py:17
  33.0 12.8 %copy-start.11 = (bf16[32,16,128]{2,1,0:T(8,128)(2,1)S(1)}, bf16[32,16,128]{2,1,0:T(8,128)(2,1)}, u32[]{:S(2)}) copy-start(bf16[32,16,128]{2,1,0:T(8,128)(2,1)} %param.11) | copy-start | bytes 393220
  46.4 0.9 copy-start.9
  48.8 1.1 copy-start.5
  49.9 23.8 %collective-permute-start.3 = (bf16[256,1024]{1,0:T(8,128)(2,1)S(1)}, bf16[256,1024]{1,0:T(8,128)(2,1)S(1)}, u32[]{:S(2)}, u32[]{:S(2)}) collective-permute-start(bf16[256,1024]{1,0:T(8,128)(2,1)S(1)} %get-tuple-element.99), channel_id=1, source_target_pairs={{1,0},{2,1},{3,2},{4,3},{5,4},{6,5},{7,6},{8,7},{9,8},{10,9},{11,1... | collective-permute-start | bytes 1572872 | tf_op jit(solution)/shard_map/ppermute | solution.py:18
  51.8 30.7 %collective-permute-start.2 = (bf16[256,1024]{1,0:T(8,128)(2,1)S(1)}, bf16[256,1024]{1,0:T(8,128)(2,1)S(1)}, u32[]{:S(2)}, u32[]{:S(2)}) collective-permute-start(bf16[256,1024]{1,0:T(8,128)(2,1)S(1)} %get-tuple-element.98), channel_id=1, source_target_pairs={{0,1},{1,2},{2,3},{3,4},{4,5},{5,6},{6,7},{7,8},{8,9},{9,10},{10,1... | collective-permute-start | bytes 1572872 | tf_op jit(solution)/shard_map/ppermute | solution.py:17
  128.2 6.9 %copy-start.10 = (bf16[1024,3072]{1,0:T(8,128)(2,1)S(1)}, bf16[1024,3072]{1,0:T(8,128)(2,1)}, u32[]{:S(2)}) copy-start(bf16[1024,3072]{1,0:T(8,128)(2,1)} %all-gather.3.cloned.1.call-done) | copy-start | bytes 18874372
  132.9 2.0 copy-start.3
  134.9 1.2 copy-start.6
  139.5 3.0 %copy-start.2 = (f32[512,3072]{1,0:T(8,128)}, f32[512,3072]{1,0:T(8,128)S(1)}, u32[]{:S(2)}) copy-start(f32[512,3072]{1,0:T(8,128)S(1)} %fusion.24) | copy-start | bytes 18874372
  176.5 1.2 copy-start.4
  197.8 6.5 %copy-start.7 = (bf16[8,512,128]{1,2,0:T(8,128)(2,1)S(1)}, bf16[8,512,128]{1,2,0:T(8,128)(2,1)}, u32[]{:S(2)}) copy-start(bf16[8,512,128]{1,2,0:T(8,128)(2,1)} %custom-call.2) | copy-start | bytes 3145732
  239.3 3.9 %copy-start.1 = (bf16[100,1024]{1,0:T(8,128)(2,1)S(1)}, bf16[100,1024]{1,0:T(8,128)(2,1)}, u32[]{:S(2)}) copy-start(bf16[100,1024]{1,0:T(8,128)(2,1)} %param.12) | copy-start | bytes 614404
Sparse Core Ops, SparseCore 0:
  10.1 118.0 all-gather.2
  130.3 82.7 all-gather.4
where the time goes:
time: 251 us; the launch traced here: 250 us
  waiting for transfers between devices  89.3 us (36%)
  local copies, waits for them, and re-layouts  62.7 us (25%)
  other arithmetic  37.6 us (15%)
  matrix products  27.6 us (11%)
  between operations  14.3 us (6%)
  starting transfers between devices  12.8 us (5%)
  loops' own time  5.75 us (2%)
    all_gather x1, waiting for transfers between devices, shards(): lax.all_gather(w_qkv, 'dp', axis=0, tiled=True)  45.7 us
    ppermute x2, waiting for transfers between devices, padded(): after = lax.ppermute(first, axis, down)  21.8 us
    ppermute x2, waiting for transfers between devices, padded(): before = lax.ppermute(last, axis, up)  21.1 us
    concatenate x1, other arithmetic, shards(): jnp.concatenate([side_pairs[:margin], own_pairs, side_pairs[margin:]], ax...  20.1 us
    gather x2, local copies, waits for them, and re-layouts, shards(): picked = jnp.take(extended, cell_index, axis=1)  12.8 us
    div x6, local copies, waits for them, and re-layouts, unit_heads(): head_rows / scale_rows  11.2 us
    dynamic_slice x8, local copies, waits for them, and re-layouts, attend(): lax.dynamic_slice_in_dim(window, offset, group_width, 1)  8.56 us
    unnamed x25, local copies, waits for them, and re-layouts  8.42 us
  transfers between devices with their start and end apart: 6, of which 5 were waited for; matrix products, arithmetic and copies ran while one was open for 47% of the time, Pallas kernels for 0%

commit v1 on v0

--- a/solution.py
+++ b/solution.py
@@ -3,8 +3,21 @@
 import jax.numpy as jnp
 from jax import lax
 from jax.sharding import PartitionSpec as P
+from jax.lax import all_to_all, axis_size
 
 HEADS = 16
+
+
+def obtain_the_side(raw, a_name):
+    return jnp.concatenate(
+        all_to_all(
+            jnp.stack(tuple((raw for _ in range(axis_size(a_name))))),
+            a_name,
+            concat_axis=0,
+            split_axis=0,
+        ),
+        axis=0,
+    )
 
 
 def padded(array, sides, width):
@@ -30,7 +43,7 @@
 def shards(fields, cell_index, interp_weight, w_in, ln_gain, w_qkv, w_out):
     width = w_qkv.shape[1] // 3
     full_qkv, full_out = (
-        lax.all_gather(w_qkv, "dp", axis=0, tiled=True),
+        obtain_the_side(w_qkv, "dp"),
         lax.all_gather(w_out, "dp", axis=0, tiled=True),
     )
     grid_field = fields[0]

time: 251 us -> 329 us (1.31)
  the two profiles are of different devices: /device:TPU:256 before, /device:TPU:460 now
where the time goes in v1:
time: 329 us; the launch traced here: 328 us
  waiting for transfers between devices  143 us (43%)
  local copies, waits for them, and re-layouts  73.2 us (22%)
  other arithmetic  40.2 us (12%)
  matrix products  29.6 us (9%)
  starting transfers between devices  22 us (7%)
  between operations  14.3 us (4%)
  loops' own time  5.72 us (2%)
    ppermute x2, waiting for transfers between devices, padded(): after = lax.ppermute(first, axis, down)  108 us
    all_to_all x1, waiting for transfers between devices, obtain_the_side(): all_to_all(jnp.stack(tuple((raw for _ in range(axis_size(a_name))))), a_n...  29.1 us
    concatenate x1, other arithmetic, shards(): jnp.concatenate([side_pairs[:margin], own_pairs, side_pairs[margin:]], ax...  20.4 us
    div x6, local copies, waits for them, and re-layouts, unit_heads(): head_rows / scale_rows  13.6 us
    gather x2, local copies, waits for them, and re-layouts, shards(): picked = jnp.take(extended, cell_index, axis=1)  12.8 us
    ppermute x2, starting transfers between devices, padded(): after = lax.ppermute(first, axis, down)  10.1 us
    mul x3, local copies, waits for them, and re-layouts, unit_heads(): head_rows * head_rows  8.77 us
    dynamic_slice x8, local copies, waits for them, and re-layouts, attend(): lax.dynamic_slice_in_dim(window, offset, group_width, 1)  8.56 us
  transfers between devices with their start and end apart: 6, of which 5 were waited for; matrix products, arithmetic and copies ran while one was open for 40% of the time, Pallas kernels for 0%

profile of v1, /device:TPU:460, one launch (start us, length us, event | category | flops | bytes accessed | tf_op | source)
XLA Modules:
  0.0 328.1 jit_solution(5546577344834277139)
XLA Ops:
  7.2 4.5 %stack.2 = bf16[16,64,3072]{2,1,0:T(8,128)(2,1)} broadcast(bf16[64,3072]{1,0:T(8,128)(2,1)} %param.14), dimensions={1,2} | broadcast | bytes 6684672 | tf_op jit(solution)/shard_map/stack | solution.py:14
  11.7 7.9 %all-to-all-start = ((bf16[16,64,3072]{2,1,0:T(8,128)(2,1)}), bf16[16,64,3072]{2,1,0:T(8,128)(2,1)}, u32[]{:S(2)}, u32[]{:S(2)}) async-start(bf16[16,64,3072]{2,1,0:T(8,128)(2,1)} %stack.2), calls=%async_computation | async-start | bytes 12582912 | tf_op jit(solution)/shard_map/all_to_all | solution.py:13
  20.3 3.9 %collective-permute-start.1 = (bf16[100,1024]{0,1:T(8,128)(2,1)S(1)}, bf16[100,1024]{0,1:T(8,128)(2,1)S(1)}, u32[]{:S(2)}, u32[]{:S(2)}) collective-permute-start(bf16[100,1024]{0,1:T(8,128)(2,1)S(1)} %get-tuple-element.101), channel_id=1, source_target_pairs={{1,0},{2,1},{3,2},{4,3},{5,4},{6,5},{7,6},{8,7},{9,8},{10,9},{11,1... | collective-permute-start | bytes 614408 | tf_op jit(solution)/shard_map/ppermute | solution.py:31
  24.3 1.9 collective-permute-start
  26.2 74.8 %collective-permute-done.1 = bf16[100,1024]{0,1:T(8,128)(2,1)S(1)} collective-permute-done((bf16[100,1024]{0,1:T(8,128)(2,1)S(1)}, bf16[100,1024]{0,1:T(8,128)(2,1)S(1)}, u32[]{:S(2)}, u32[]{:S(2)}) %collective-permute-start.1) | collective-permute-done | bytes 204832 | tf_op jit(solution)/shard_map/ppermute | solution.py:31
  101.0 2.6 collective-permute-done
  103.9 12.1 %gather_fusion = bf16[4096,100]{1,0:T(8,128)(2,1)S(1)} fusion(bf16[100,6144]{0,1:T(8,128)(2,1)S(1)} %pad_maximum_fusion, s32[4096]{0:T(1024)S(1)} %bitcast_clamp_fusion), kind=kCustom, calls=%fused_computation | custom fusion | bytes 1654784 | tf_op jit(solution)/shard_map/jit(_take)/gather | solution.py:53
  119.7 6.2 %collective-permute-start.3 = (bf16[256,1024]{1,0:T(8,128)(2,1)S(1)}, bf16[256,1024]{1,0:T(8,128)(2,1)S(1)}, u32[]{:S(2)}, u32[]{:S(2)}) collective-permute-start(bf16[256,1024]{1,0:T(8,128)(2,1)S(1)} %get-tuple-element.99), channel_id=1, source_target_pairs={{1,0},{2,1},{3,2},{4,3},{5,4},{6,5},{7,6},{8,7},{9,8},{10,9},{11,1... | collective-permute-start | bytes 1572872 | tf_op jit(solution)/shard_map/ppermute | solution.py:31
  125.9 2.1 collective-permute-start.2
  128.0 32.7 %collective-permute-done.3 = bf16[256,1024]{1,0:T(8,128)(2,1)S(1)} collective-permute-done((bf16[256,1024]{1,0:T(8,128)(2,1)S(1)}, bf16[256,1024]{1,0:T(8,128)(2,1)S(1)}, u32[]{:S(2)}, u32[]{:S(2)}) %collective-permute-start.3) | collective-permute-done | bytes 524320 | tf_op jit(solution)/shard_map/ppermute | solution.py:31
  160.7 3.8 %collective-permute-done.2 = bf16[256,1024]{1,0:T(8,128)(2,1)S(1)} collective-permute-done((bf16[256,1024]{1,0:T(8,128)(2,1)S(1)}, bf16[256,1024]{1,0:T(8,128)(2,1)S(1)}, u32[]{:S(2)}, u32[]{:S(2)}) %collective-permute-start.2) | collective-permute-done | bytes 524320 | tf_op jit(solution)/shard_map/ppermute | solution.py:30
  164.6 29.1 %all-to-all-done = bf16[16,64,3072]{2,1,0:T(8,128)(2,1)} async-done(((bf16[16,64,3072]{2,1,0:T(8,128)(2,1)}), bf16[16,64,3072]{2,1,0:T(8,128)(2,1)}, u32[]{:S(2)}, u32[]{:S(2)}) %all-to-all-start) | async-done | bytes 6291488 | tf_op jit(solution)/shard_map/all_to_all | solution.py:13
  193.6 4.5 %fusion.8 = f32[512,2048]{1,0:T(8,128)S(1)} fusion(bf16[1024,3072]{1,0:T(8,128)(2,1)} %bitcast.13, bf16[256,1024]{1,0:T(8,128)(2,1)S(1)} %collective-permute-done.3, bf16[256,1024]{1,0:T(8,128)(2,1)S(1)} %collective-permute-done.2), kind=kOutput, calls=%fused_computation.16 | convolution fusion | flops 2149580800 | bytes 9437184 | tf_op jit(solution)/shard_map/dot_general | solution.py:66
  198.4 1.9 copy-done.3
  201.8 5.5 %fusion.24 = f32[512,3072]{1,0:T(8,128)S(1)} fusion(bf16[512,1024]{1,0:T(8,128)(2,1)S(1)} %get-tuple-element.96, bf16[1024,3072]{1,0:T(8,128)(2,1)} %bitcast.13), kind=kOutput, calls=%fused_computation.59 | convolution fusion | flops 3221225472 | bytes 13631488 | tf_op jit(solution)/shard_map/dot_general | solution.py:65
  207.5 2.5 copy-done.2
  210.0 2.4 slice_multiply_fusion
  212.4 2.9 copy.15
  215.3 1.9 bitcast_reduce_fusion.2
  218.8 2.9 copy.16
  221.7 2.6 divide_convert_fusion.6
  224.4 2.9 copy.19
  227.3 1.9 bitcast_reduce_fusion
  230.8 2.9 copy.20
  233.7 2.9 copy.17
  236.7 1.9 bitcast_reduce_fusion.1
  240.2 2.9 copy.18
  243.1 5.3 %divide_convert_fusion.4 = (bf16[512,1024]{1,0:T(8,128)(2,1)}, bf16[512,1024]{1,0:T(8,128)(2,1)S(1)}) fusion(f32[512,1024]{1,0:T(8,128)} %copy.20, f32[512,3072]{1,0:T(8,128)} %copy-done.2, f32[512,1024]{1,0:T(8,128)} %copy.18), kind=kLoop, calls=%fused_computation.25 | loop fusion | flops 2097152 | bytes 10485760 | tf_op jit(solution)/shard_map/convert_element_type | solution.py:40
  248.5 20.4 %fusion.7 = bf16[1024,2048]{1,0:T(8,128)(2,1)} fusion(bf16[512,1024]{1,0:T(8,128)(2,1)S(1)} %slice.81, bf16[512,1024]{1,0:T(8,128)(2,1)S(1)} %divide_convert_fusion.6, bf16[512,1024]{1,0:T(8,128)(2,1)S(1)} %slice.80, bf16[512,1024]{1,0:T(8,128)(2,1)S(1)} %get-tuple-element.93, bf16[256,2048]{1,0:T(8,128)(2,1)S(1)} %fusion.11), kind=kLoop, calls=%fused_computation.15 | loop fusion | flops 27262976 | bytes 9437184 | tf_op jit(solution)/shard_map/concatenate | solution.py:79
  268.9 6.5 %copy.21 = bf16[1024,2048]{0,1:T(8,128)(2,1)} copy(bf16[1024,2048]{1,0:T(8,128)(2,1)} %fusion.7) | data formatting | bytes 8388608 | tf_op jit(solution)/shard_map/while | solution.py:104
  275.4 41.9 %while.12 = (s32[]{:T(128)}, bf16[8,512,128]{1,2,0:T(8,128)(2,1)S(1)}, s32[8]{0:T(128)S(1)}, bf16[1024,2048]{0,1:T(8,128)(2,1)}, bf16[512,1024]{1,0:T(8,128)(2,1...) while((s32[]{:T(128)}, ...), condition=%wide.region_7.8_spmd, body=%wide.region_5.7_spmd.sunk | while | flops 273742848 | bytes 11018490 | solution.py:104
  317.4 3.9 %fusion.10 = bf16[1,512,1024]{2,1,0:T(8,128)(2,1)} fusion(bf16[512,1024]{0,1:T(8,128)(2,1)S(1)} %bitcast.70, bf16[1024,1024]{1,0:T(8,128)(2,1)} %all-gather.2.cloned.1.call-done), kind=kOutput, calls=%fused_computation.35 | convolution fusion | flops 1074266112 | bytes 4194304 | tf_op jit(solution)/shard_map/dot_general | solution.py:106
  (100 shorter events, 47.8 us)
Async XLA Ops:
  7.2 110.1 %copy-start = (bf16[100,1024]{1,0:T(8,128)(2,1)S(1)}, bf16[100,1024]{1,0:T(8,128)(2,1)}, u32[]{:S(2)}) copy-start(bf16[100,1024]{1,0:T(8,128)(2,1)} %param.12) | copy-start | bytes 614404
  11.7 7.9 %copy-start.5 = (bf16[1,100,4096]{2,1,0:T(8,128)(2,1)S(1)}, bf16[1,100,4096]{2,1,0:T(8,128)(2,1)}, u32[]{:S(2)}) copy-start(bf16[1,100,4096]{2,1,0:T(8,128)(2,1)} %param.9) | copy-start | bytes 2457604
  11.7 182.0 %all-to-all-start = ((bf16[16,64,3072]{2,1,0:T(8,128)(2,1)}), bf16[16,64,3072]{2,1,0:T(8,128)(2,1)}, u32[]{:S(2)}, u32[]{:S(2)}) async-start(bf16[16,64,3072]{2,1,0:T(8,128)(2,1)} %stack.2), calls=%async_computation | async-start | bytes 12582912 | tf_op jit(solution)/shard_map/all_to_all | solution.py:13
  19.5 6.7 %copy-start.6 = (s32[32,128]{1,0:T(8,128)S(1)}, s32[32,128]{1,0:T(8,128)}, u32[]{:S(2)}) copy-start(s32[32,128]{1,0:T(8,128)} %param.10) | copy-start | bytes 49156
  19.5 297.8 %all-gather.2.cloned.1.call-start = ((), (), s32[]{:S(2)}) async-start(), calls=%async_computation.1 | async-start | bytes 2228224 | tf_op jit(solution)/shard_map/all_gather | solution.py:47
  20.3 80.7 %collective-permute-start.1 = (bf16[100,1024]{0,1:T(8,128)(2,1)S(1)}, bf16[100,1024]{0,1:T(8,128)(2,1)S(1)}, u32[]{:S(2)}, u32[]{:S(2)}) collective-permute-start(bf16[100,1024]{0,1:T(8,128)(2,1)S(1)} %get-tuple-element.101), channel_id=1, source_target_pairs={{1,0},{2,1},{3,2},{4,3},{5,4},{6,5},{7,6},{8,7},{9,8},{10,9},{11,1... | collective-permute-start | bytes 614408 | tf_op jit(solution)/shard_map/ppermute | solution.py:31
  24.3 79.3 %collective-permute-start = (bf16[100,1024]{0,1:T(8,128)(2,1)S(1)}, bf16[100,1024]{0,1:T(8,128)(2,1)S(1)}, u32[]{:S(2)}, u32[]{:S(2)}) collective-permute-start(bf16[100,1024]{0,1:T(8,128)(2,1)S(1)} %get-tuple-element.100), channel_id=1, source_target_pairs={{0,1},{1,2},{2,3},{3,4},{4,5},{5,6},{6,7},{7,8},{8,9},{9,10},{10,1... | collective-permute-start | bytes 614408 | tf_op jit(solution)/shard_map/ppermute | solution.py:30
  103.9 12.8 %copy-start.8 = (bf16[32,16,128]{2,1,0:T(8,128)(2,1)S(1)}, bf16[32,16,128]{2,1,0:T(8,128)(2,1)}, u32[]{:S(2)}) copy-start(bf16[32,16,128]{2,1,0:T(8,128)(2,1)} %param.11) | copy-start | bytes 393220
  117.3 0.9 copy-start.7
  119.7 41.0 %collective-permute-start.3 = (bf16[256,1024]{1,0:T(8,128)(2,1)S(1)}, bf16[256,1024]{1,0:T(8,128)(2,1)S(1)}, u32[]{:S(2)}, u32[]{:S(2)}) collective-permute-start(bf16[256,1024]{1,0:T(8,128)(2,1)S(1)} %get-tuple-element.99), channel_id=1, source_target_pairs={{1,0},{2,1},{3,2},{4,3},{5,4},{6,5},{7,6},{8,7},{9,8},{10,9},{11,1... | collective-permute-start | bytes 1572872 | tf_op jit(solution)/shard_map/ppermute | solution.py:31
  125.9 38.7 %collective-permute-start.2 = (bf16[256,1024]{1,0:T(8,128)(2,1)S(1)}, bf16[256,1024]{1,0:T(8,128)(2,1)S(1)}, u32[]{:S(2)}, u32[]{:S(2)}) collective-permute-start(bf16[256,1024]{1,0:T(8,128)(2,1)S(1)} %get-tuple-element.98), channel_id=1, source_target_pairs={{0,1},{1,2},{2,3},{3,4},{4,5},{5,6},{6,7},{7,8},{8,9},{9,10},{10,1... | collective-permute-start | bytes 1572872 | tf_op jit(solution)/shard_map/ppermute | solution.py:30
  198.2 2.0 copy-start.3
  207.3 2.7 copy-start.2
  268.9 6.5 %copy-start.4 = (bf16[8,512,128]{1,2,0:T(8,128)(2,1)S(1)}, bf16[8,512,128]{1,2,0:T(8,128)(2,1)}, u32[]{:S(2)}) copy-start(bf16[8,512,128]{1,2,0:T(8,128)(2,1)} %custom-call.2) | copy-start | bytes 3145732
  317.3 3.9 %copy-start.1 = (bf16[100,1024]{1,0:T(8,128)(2,1)S(1)}, bf16[100,1024]{1,0:T(8,128)(2,1)}, u32[]{:S(2)}) copy-start(bf16[100,1024]{1,0:T(8,128)(2,1)} %param.12) | copy-start | bytes 614404
Sparse Core Ops, SparseCore 0:
  128.1 121.1 all-gather.1
